TPU v7x, 32 devices: a whole 2x2x4 slice. The times are simulated.
32 devices in a mesh: groups: 2 (over y), dp: 4 (over z), mp: 4 (over x, core).
Axes of the slice: x: 2, y: 2, z: 4, core: 2. Of those that a mesh axis runs over, the one named last changes fastest.
Arguments:
- tokens: bfloat16 [1024, 7168], P(('groups', 'dp')), parts along dimension 0, may hold values from -20 to 20, as said below
- w_down: bfloat16 [7168, 1536], P('dp', 'mp'), may hold values from -3 to 3, as said below
- gain: float32 [1536], P('mp'), may hold values from 0.25 to 1.75
- w_up: bfloat16 [1536, 26112], P('dp', 'mp'), may hold values from -0.15625 to 0.15625
- head_counts: int32 [4], replicated, may hold values from 30 to 34, as said below
- cotangent: bfloat16 [1024, 26112], P(('groups', 'dp'), 'mp'), parts along dimension 0, may hold values from -6 to 6
Outputs:
- queries: bfloat16 [1024, 26112], P(('groups', 'dp'), 'mp'), parts along dimension 0
- grad_tokens: bfloat16 [1024, 7168], P(('groups', 'dp'), 'mp'), parts along dimension 0
There are 2 independent parts, one for each index of `groups`. A program takes and returns all parts, laid end to end along the dimension named above; an argument that names none is the same for every part. Nothing has to cross between parts.
Inputs may be any that keep to these rules, and one draw needn't show every extreme that they name: `tokens`: hidden states of order one with token scales that differ. `w_down`: entries of order 7168^(-1/2). `head_counts`: the entries sum to 128; one of them is 34.
All inputs are finite; a program needn't handle non-finite values.
Results may differ from a plain program's by a relative error of at most 0.018.
Values may be sent and summed in bfloat16 or wider, within the bound.
A program may use at most 128 MiB of HBM per device.

v0:
```python
import jax
import jax.numpy as jnp
from jax import lax
from jax.sharding import PartitionSpec as P

HD = 192


def contract_last(left, right):
    return lax.dot_general(
        left, right, (((1,), (1,)), ((), ())), preferred_element_type=jnp.float32
    )


def keep_mask_of(head_counts, block_cols):
    position = lax.axis_index("mp")
    held_heads = lax.dynamic_slice_in_dim(head_counts, position, 1, 0)
    slot_index = jnp.arange(block_cols, dtype=jnp.int32) // HD
    return (slot_index < held_heads).astype(jnp.float32)


def gather_weights_body(tokens, w_down, gain, w_up, head_counts, cotangent):
    latent_width = w_down.shape[1] * lax.axis_size("mp")
    keep_mask = keep_mask_of(head_counts, w_up.shape[1])
    down_whole = lax.all_gather(w_down, "dp", axis=0, tiled=True)
    latent_raw = jnp.dot(tokens, down_whole, preferred_element_type=jnp.float32)
    squares = lax.psum(jnp.sum(latent_raw * latent_raw, axis=1, keepdims=True), "mp")
    root_mean = jnp.sqrt(squares / latent_width + 1e-06)
    latent_local = (latent_raw / root_mean * gain).astype(jnp.bfloat16)
    latent = lax.all_gather(latent_local, "mp", axis=1, tiled=True)
    masked = cotangent * keep_mask.astype(jnp.bfloat16)
    up_whole = lax.all_gather(w_up, "dp", axis=0, tiled=True)
    query_total = jnp.dot(latent, up_whole, preferred_element_type=jnp.float32)
    grad_partial = contract_last(masked, up_whole)
    queries = (query_total * keep_mask).astype(jnp.bfloat16)
    grad_latent = lax.psum_scatter(
        grad_partial.astype(jnp.bfloat16), "mp", scatter_dimension=1, tiled=True
    ).astype(jnp.float32)
    inner_dot = lax.psum(jnp.sum(gain * grad_latent * latent_raw, axis=1, keepdims=True), "mp")
    grad_raw = (
        gain * grad_latent / root_mean - latent_raw * inner_dot / (latent_width * root_mean**3)
    ).astype(jnp.bfloat16)
    partial_value = contract_last(grad_raw, down_whole).astype(jnp.bfloat16)
    grad_tokens = lax.psum_scatter(partial_value, "mp", scatter_dimension=1, tiled=True)
    return (queries, grad_tokens)


def move_tokens_body(tokens, w_down, gain, w_up, head_counts, cotangent):
    n = lax.axis_size("mp")
    swap = [(i * n + j, j * n + i) for i in range(n) for j in range(n)]
    position = lax.axis_index("mp")
    latent_width = w_down.shape[1] * n
    keep_mask = keep_mask_of(head_counts, w_up.shape[1])

    def transpose_owner(block):
        return lax.ppermute(block, ("dp", "mp"), swap)

    rows = w_down.shape[0]
    tokens_block = lax.dynamic_slice_in_dim(tokens, position * rows, rows, 1)
    tokens_cols = lax.all_gather(transpose_owner(tokens_block), "mp", axis=0, tiled=True)
    raw_partial = jnp.dot(tokens_cols, w_down, preferred_element_type=jnp.float32)
    latent_raw = lax.psum_scatter(raw_partial, "dp", scatter_dimension=0, tiled=True)
    squares = lax.psum(jnp.sum(latent_raw * latent_raw, axis=1, keepdims=True), "mp")
    root_mean = jnp.sqrt(squares / latent_width + 1e-06)
    latent_local = (latent_raw / root_mean * gain).astype(jnp.bfloat16)
    latent = lax.all_gather(transpose_owner(latent_local), "mp", axis=0, tiled=True)
    query_partial = (jnp.dot(latent, w_up, preferred_element_type=jnp.float32) * keep_mask).astype(
        jnp.bfloat16
    )
    masked = cotangent * keep_mask.astype(jnp.bfloat16)
    masked_all = lax.all_gather(masked, "dp", axis=0, tiled=True)
    queries = lax.psum_scatter(query_partial, "dp", scatter_dimension=0, tiled=True)
    grad_partial = contract_last(masked_all, w_up).astype(jnp.bfloat16)
    grad_latent = transpose_owner(
        lax.psum_scatter(grad_partial, "mp", scatter_dimension=0, tiled=True)
    ).astype(jnp.float32)
    inner_dot = lax.psum(jnp.sum(gain * grad_latent * latent_raw, axis=1, keepdims=True), "mp")
    grad_raw = (
        gain * grad_latent / root_mean - latent_raw * inner_dot / (latent_width * root_mean**3)
    ).astype(jnp.bfloat16)
    grad_raw_all = lax.all_gather(grad_raw, "dp", axis=0, tiled=True)
    token_partial = contract_last(grad_raw_all, w_down).astype(jnp.bfloat16)
    grad_tokens = transpose_owner(
        lax.psum_scatter(token_partial, "mp", scatter_dimension=0, tiled=True)
    )
    return (queries, grad_tokens)


def solution(mesh):
    in_specs = (
        P(("groups", "dp"), None),
        P("dp", "mp"),
        P("mp"),
        P("dp", "mp"),
        P(),
        P(("groups", "dp"), "mp"),
    )
    out_specs = (P(("groups", "dp"), "mp"), P(("groups", "dp"), "mp"))
    square = mesh.shape["dp"] == mesh.shape["mp"]
    body = move_tokens_body if square else gather_weights_body
    return jax.shard_map(body, mesh=mesh, in_specs=in_specs, out_specs=out_specs, check_vma=False)
```

profile of v0, /device:TPU:9, one launch (start us, length us, event | category | flops | bytes accessed | tf_op | source)
XLA Modules:
  0.0 414.5 jit_solution(11642540966179792071)
XLA Ops:
  7.2 0.0 copy-start
  7.2 0.0 all-gather.5.cloned.1.call-start
  7.2 1.3 dynamic_slice.7
  8.6 0.6 fusion.5
  9.1 2.8 broadcast_multiply_fusion
  11.9 0.0 all-gather.5.cloned.1.call-update
  11.9 0.0 all-gather.3.cloned.1.call-start
  12.0 0.0 copy-done
  12.1 0.7 collective-permute-start
  12.8 0.0 collective-permute-done
  12.8 0.0 copy-start.2
  12.8 0.8 copy-done.2
  13.5 0.0 all-gather.3.cloned.1.call-update
  13.6 0.0 copy-start.1
  13.6 0.0 reduce-scatter.9.cloned.1.call-start
  13.6 118.5 %all-gather.5.cloned.1.call-done = bf16[512,6528]{1,0:T(8,128)(2,1)} async-done(((bf16[128,6528]{1,0:T(8,128)(2,1)}), bf16[512,6528]{1,0:T(8,128)(2,1)}) %all-gather.5.cloned.1.call-update) | async-done | bytes 6684688 | tf_op jit(solution)/shard_map/all_gather | solution.py:71
  132.1 8.7 %convolution_convert_fusion.1 = bf16[512,384]{1,0:T(8,128)(2,1)} fusion(bf16[512,6528]{1,0:T(8,128)(2,1)} %all-gather.5.cloned.1.call-done, bf16[384,6528]{1,0:T(8,128)(2,1)} %param.9), kind=kOutput, calls=%fused_computation.2 | convolution fusion | flops 2567110656 | bytes 12091392 | tf_op jit(solution)/shard_map/dot_general | solution.py:10
  140.8 0.0 reduce-scatter.9.cloned.1.call-update
  140.8 0.0 copy-start.3
  140.9 0.0 reduce-scatter.5.cloned.1.call-start
  140.9 28.4 %all-gather.3.cloned.1.call-done = bf16[512,1792]{1,0:T(8,128)(2,1)} async-done(((bf16[128,1792]{1,0:T(8,128)(2,1)}), bf16[512,1792]{1,0:T(8,128)(2,1)}) %all-gather.3.cloned.1.call-update) | async-done | bytes 1835024 | tf_op jit(solution)/shard_map/all_gather | solution.py:60
  169.3 0.0 copy-done.1
  169.3 3.5 fusion.9
  172.8 0.0 reduce-scatter.5.cloned.1.call-update
  172.8 0.0 reduce-scatter.11.cloned.1.call-start
  172.9 19.2 %reduce-scatter.9.cloned.1.call-done = bf16[128,384]{1,0:T(8,128)(2,1)} async-done(((bf16[512,384]{1,0:T(8,128)(2,1)}), bf16[128,384]{1,0:T(8,128)(2,1)}) %reduce-scatter.9.cloned.1.call-update) | async-done | bytes 98320 | tf_op jit(solution)/shard_map/reduce_scatter | solution.py:75
  192.1 1.5 collective-permute-start.2
  193.7 22.3 %reduce-scatter.5.cloned.1.call-done = f32[128,384]{1,0:T(8,128)} async-done(((f32[512,384]{1,0:T(8,128)}), f32[128,384]{1,0:T(8,128)}) %reduce-scatter.5.cloned.1.call-update) | async-done | bytes 196624 | tf_op jit(solution)/shard_map/reduce_scatter | solution.py:62
  216.0 0.0 collective-permute-done.2
  216.0 0.0 copy-done.3
  216.0 1.0 multiply_reduce_fusion
  217.0 6.4 %all-reduce = (f32[128,1]{0,1:T(1,128)S(1)}, f32[128]{0:T(128)S(1)}) all-reduce(f32[128,1]{0,1:T(1,128)S(1)} %bitcast.14, f32[128]{0:T(128)S(1)} %get-tuple-element.2), channel_id=1, replica_groups=mesh['groups'=2,'dp'=4,'mp'=4] {'mp'}, use_global_device_ids=true, to_apply=%region_2.3 | all-reduce | flops 256 | bytes 2048 | tf_op jit(solution)/shard_map/psum | solution.py:63
  223.5 1.1 subtract_convert_fusion
  224.6 12.0 %all_gather.15 = bf16[512,384]{1,0:T(8,128)(2,1)S(1)} all-gather(bf16[128,384]{1,0:T(8,128)(2,1)S(1)} %get-tuple-element.6), channel_id=1, replica_groups=mesh['groups'=2,'dp'=4,'mp'=4] {'dp'}, dimensions={0}, use_global_device_ids=true | all-gather | bytes 491520 | tf_op jit(solution)/shard_map/all_gather | solution.py:81
  236.5 2.4 convolution_convert_fusion
  239.0 0.0 reduce-scatter.11.cloned.1.call-update
  239.0 0.0 reduce-scatter.7.cloned.1.call-start
  239.0 0.7 collective-permute-start.1
  239.7 0.6 fusion.3
  240.3 0.0 collective-permute-done.1
  240.3 16.2 %all_gather.13 = bf16[512,384]{1,0:T(8,128)(2,1)S(1)} all-gather(bf16[128,384]{1,0:T(8,128)(2,1)S(1)} %collective-permute-done.1), channel_id=1, replica_groups=mesh['groups'=2,'dp'=4,'mp'=4] {'mp'}, dimensions={0}, use_global_device_ids=true | all-gather | bytes 491520 | tf_op jit(solution)/shard_map/all_gather | solution.py:66
  256.4 8.0 %multiply_convert_fusion = bf16[512,6528]{1,0:T(8,128)(2,1)} fusion(bf16[512,384]{1,0:T(8,128)(2,1)S(1)} %all_gather.13, bf16[384,6528]{1,0:T(8,128)(2,1)} %param.9, f32[6528]{0:T(1024)S(1)} %fusion.3), kind=kOutput, calls=%fused_computation | convolution fusion | flops 2573598720 | bytes 12117504 | tf_op jit(solution)/shard_map/dot_general | solution.py:67
  264.5 0.0 reduce-scatter.7.cloned.1.call-update
  264.5 8.1 %reduce-scatter.11.cloned.1.call-done = bf16[128,1792]{1,0:T(8,128)(2,1)} async-done(((bf16[512,1792]{1,0:T(8,128)(2,1)}), bf16[128,1792]{1,0:T(8,128)(2,1)}) %reduce-scatter.11.cloned.1.call-update) | async-done | bytes 458768 | tf_op jit(solution)/shard_map/reduce_scatter | solution.py:84
  272.5 1.7 collective-permute-start.3
  274.2 0.0 collective-permute-done.3
  274.2 132.7 %reduce-scatter.7.cloned.1.call-done = bf16[128,6528]{1,0:T(8,128)(2,1)} async-done(((bf16[512,6528]{1,0:T(8,128)(2,1)}), bf16[128,6528]{1,0:T(8,128)(2,1)}) %reduce-scatter.7.cloned.1.call-update) | async-done | bytes 1671184 | tf_op jit(solution)/shard_map/reduce_scatter | solution.py:72
  406.9 0.8 copy.9
  (2 shorter events, 0.1 us)
Async XLA Ops:
  7.2 4.8 %copy-start = (bf16[128,7168]{1,0:T(8,128)(2,1)S(1)}, bf16[128,7168]{1,0:T(8,128)(2,1)}, u32[]{:S(2)}) copy-start(bf16[128,7168]{1,0:T(8,128)(2,1)} %param.6) | copy-start | bytes 5505028
  7.2 124.9 %all-gather.5.cloned.1.call-start = ((), (), s32[]{:S(2)}) async-start(), calls=%async_computation.7 | async-start | bytes 8355840 | tf_op jit(solution)/shard_map/all_gather | solution.py:71
  11.9 157.4 %all-gather.3.cloned.1.call-start = ((), (), s32[]{:S(2)}) async-start(), calls=%async_computation.4 | async-start | bytes 2293760 | tf_op jit(solution)/shard_map/all_gather | solution.py:60
  12.1 0.7 collective-permute-start
  12.8 0.8 copy-start.2
  13.6 155.8 %copy-start.1 = (bf16[1792,384]{1,0:T(8,128)(2,1)S(1)}, bf16[1792,384]{1,0:T(8,128)(2,1)}, u32[]{:S(2)}) copy-start(bf16[1792,384]{1,0:T(8,128)(2,1)} %param.7) | copy-start | bytes 4128772
  13.6 178.5 %reduce-scatter.9.cloned.1.call-start = ((), (), s32[]{:S(2)}) async-start(), calls=%async_computation.8 | async-start | bytes 491520 | tf_op jit(solution)/shard_map/reduce_scatter | solution.py:75
  140.8 75.2 %copy-start.3 = (f32[384]{0:T(512)S(1)}, f32[384]{0:T(512)}, u32[]{:S(2)}) copy-start(f32[384]{0:T(512)} %param.8) | copy-start | bytes 4612
  140.9 75.1 %reduce-scatter.5.cloned.1.call-start = ((), (), s32[]{:S(2)}) async-start(), calls=%async_computation.5 | async-start | bytes 983040 | tf_op jit(solution)/shard_map/reduce_scatter | solution.py:62
  172.8 99.7 %reduce-scatter.11.cloned.1.call-start = ((), (), s32[]{:S(2)}) async-start(), calls=%async_computation.9 | async-start | bytes 2293760 | tf_op jit(solution)/shard_map/reduce_scatter | solution.py:84
  192.1 23.9 %collective-permute-start.2 = (bf16[128,384]{1,0:T(8,128)(2,1)}, bf16[128,384]{1,0:T(8,128)(2,1)S(1)}, u32[]{:S(2)}, u32[]{:S(2)}) collective-permute-start(bf16[128,384]{1,0:T(8,128)(2,1)} %reduce-scatter.9.cloned.1.call-done), channel_id=1, source_target_pairs={{0,0},{1,4},{2,8},{3,12},{4,1},{5,5},{6,9},{7,13},{8,2},{9,6},{10,... | collective-permute-start | bytes 294920 | tf_op jit(solution)/shard_map/ppermute | solution.py:56
  239.0 167.9 %reduce-scatter.7.cloned.1.call-start = ((), (), s32[]{:S(2)}) async-start(), calls=%async_computation.6 | async-start | bytes 8355840 | tf_op jit(solution)/shard_map/reduce_scatter | solution.py:72
  239.0 1.2 collective-permute-start.1
  272.5 1.7 collective-permute-start.3
Sparse Core Ops, SparseCore 0:
  12.1 119.9 all-gather.4
  134.2 35.0 all-gather.2
  171.8 20.2 reduce-scatter.8
  194.8 21.1 reduce-scatter.4
  239.1 33.3 reduce-scatter.10
  275.3 131.5 reduce-scatter.6
where the time goes:
time: 415 us
  waiting for transfers between devices  329 us (79%)
  blocking collectives  34.6 us (8%)
  matrix products  22.7 us (5%)
  between operations  14.2 us (3%)
  other arithmetic  6.03 us (1%)
  starting transfers between devices  4.8 us (1%)
    reduce_scatter x1, waiting for transfers between devices, move_tokens_body(): lax.psum_scatter(query_partial, 'dp', scatter_dimension=0, tiled=True)  133 us
    all_gather x1, waiting for transfers between devices, move_tokens_body(): masked_all = lax.all_gather(masked, 'dp', axis=0, tiled=True)  118 us
    all_gather x1, waiting for transfers between devices, move_tokens_body(): lax.all_gather(transpose_owner(tokens_block), 'mp', axis=0, tiled=True)  28.4 us
    reduce_scatter x1, waiting for transfers between devices, move_tokens_body(): lax.psum_scatter(raw_partial, 'dp', scatter_dimension=0, tiled=True)  22.3 us
    reduce_scatter x1, waiting for transfers between devices, move_tokens_body(): lax.psum_scatter(grad_partial, 'mp', scatter_dimension=0, tiled=True)  19.2 us
    all_gather x1, blocking collectives, move_tokens_body(): lax.all_gather(transpose_owner(latent_local), 'mp', axis=0, tiled=True)  16.2 us
    all_gather x1, blocking collectives, move_tokens_body(): grad_raw_all = lax.all_gather(grad_raw, 'dp', axis=0, tiled=True)  12 us
    dot_general x2, matrix products, contract_last(): lax.dot_general(left, right, (((1,), (1,)), ((), ())), preferred_element_...  11.2 us
  transfers between devices with their start and end apart: 10, of which 6 were waited for; matrix products, arithmetic and copies ran while one was open for 5% of the time, Pallas kernels for 0%

commit v1 on v0

--- a/solution.py
+++ b/solution.py
@@ -68,7 +68,12 @@
         jnp.bfloat16
     )
     masked = cotangent * keep_mask.astype(jnp.bfloat16)
-    masked_all = lax.all_gather(masked, "dp", axis=0, tiled=True)
+    ring = [masked]
+    for hop in range(3):
+        ring.append(lax.ppermute(ring[-1], "dp", [(dev, (dev + 1) % 4) for dev in range(4)]))
+    masked_all = jnp.roll(
+        jnp.concatenate(ring[::-1], axis=0), (lax.axis_index("dp") + 1) * ring[0].shape[0], axis=0
+    )
     queries = lax.psum_scatter(query_partial, "dp", scatter_dimension=0, tiled=True)
     grad_partial = contract_last(masked_all, w_up).astype(jnp.bfloat16)
     grad_latent = transpose_owner(

time: 415 us -> 415 us (level)
  waiting for transfers between devices: 329 us -> 320 us
  local copies, waits for them, and re-layouts: 2.92 us -> 10.4 us
  starting transfers between devices: 4.8 us -> 11.8 us
  matrix products: 22.7 us -> 18.3 us
    all_gather x1 -> x0, waiting for transfers between devices: 118 us -> none  [move_tokens_body(): masked_all = lax.all_gather(masked, 'dp', axis=0, tiled=True)]
    ppermute x0 -> x3, waiting for transfers between devices: none -> 105 us  [move_tokens_body(): lax.ppermute(ring[-1], 'dp', [(dev, (dev + 1) % 4) for dev in range(4)])]
    unnamed x9 -> x19, local copies, waits for them, and re-layouts: 1.55 us -> 8.15 us
    ppermute x4, starting transfers between devices: 4.56 us -> 8.92 us  [transpose_owner(): return lax.ppermute(block, ('dp', 'mp'), swap)]
    dot_general x2, matrix products: 11.2 us -> 6.83 us  [contract_last(): lax.dot_general(left, right, (((1,), (1,)), ((), ())), preferred_element_...]
  transfers between devices with their start and end apart: 10 -> 12, of which waited for: 6 -> 8; matrix products, arithmetic and copies ran while one was open for 5% -> 6% of each run, Pallas kernels for 0% -> 0%
where the time goes in v1:
time: 415 us; the launch traced here: 414 us
  waiting for transfers between devices  320 us (77%)
  blocking collectives  34.4 us (8%)
  matrix products  18.3 us (4%)
  between operations  13.9 us (3%)
  starting transfers between devices  11.8 us (3%)
  local copies, waits for them, and re-layouts  10.4 us (3%)
  other arithmetic  5.85 us (1%)
    reduce_scatter x1, waiting for transfers between devices, move_tokens_body(): lax.psum_scatter(query_partial, 'dp', scatter_dimension=0, tiled=True)  133 us
    ppermute x3, waiting for transfers between devices, move_tokens_body(): lax.ppermute(ring[-1], 'dp', [(dev, (dev + 1) % 4) for dev in range(4)])  105 us
    all_gather x1, waiting for transfers between devices, move_tokens_body(): lax.all_gather(transpose_owner(tokens_block), 'mp', axis=0, tiled=True)  31.4 us
    reduce_scatter x1, waiting for transfers between devices, move_tokens_body(): lax.psum_scatter(raw_partial, 'dp', scatter_dimension=0, tiled=True)  22.5 us
    reduce_scatter x1, waiting for transfers between devices, move_tokens_body(): lax.psum_scatter(grad_partial, 'mp', scatter_dimension=0, tiled=True)  19.8 us
    all_gather x1, blocking collectives, move_tokens_body(): lax.all_gather(transpose_owner(latent_local), 'mp', axis=0, tiled=True)  16 us
    all_gather x1, blocking collectives, move_tokens_body(): grad_raw_all = lax.all_gather(grad_raw, 'dp', axis=0, tiled=True)  11.9 us
    ppermute x4, starting transfers between devices, transpose_owner(): return lax.ppermute(block, ('dp', 'mp'), swap)  8.92 us
  transfers between devices with their start and end apart: 12, of which 8 were waited for; matrix products, arithmetic and copies ran while one was open for 6% of the time, Pallas kernels for 0%

profile of v1, /device:TPU:9, one launch (start us, length us, event | category | flops | bytes accessed | tf_op | source)
XLA Modules:
  0.0 414.3 jit_solution(5221564843015203035)
XLA Ops:
  7.2 0.0 copy-start
  7.2 0.0 all-gather.2.cloned.1.call-start
  7.2 1.4 dynamic_slice.11
  8.7 0.7 fusion.10
  9.4 1.6 broadcast_multiply_fusion
  11.0 1.3 collective-permute-start.2
  12.4 36.1 %collective-permute-done.2 = bf16[128,6528]{1,0:T(8,128)(2,1)S(1)} collective-permute-done((bf16[128,6528]{1,0:T(8,128)(2,1)S(1)}, bf16[128,6528]{1,0:T(8,128)(2,1)S(1)}, u32[]{:S(2)}, u32[]{:S(2)}) %collective-permute-start.2) | collective-permute-done | bytes 1671200 | tf_op jit(solution)/shard_map/ppermute | solution.py:73
  48.4 1.3 collective-permute-start.3
  49.7 36.7 %collective-permute-done.3 = bf16[128,6528]{1,0:T(8,128)(2,1)} collective-permute-done((bf16[128,6528]{1,0:T(8,128)(2,1)S(1)}, bf16[128,6528]{1,0:T(8,128)(2,1)}, u32[]{:S(2)}, u32[]{:S(2)}) %collective-permute-start.3) | collective-permute-done | bytes 1671200 | tf_op jit(solution)/shard_map/ppermute | solution.py:73
  86.5 0.8 constant_dynamic-slice_fusion
  87.3 5.1 %collective-permute-start = (bf16[128,1792]{1,0:T(8,128)(2,1)}, bf16[128,1792]{1,0:T(8,128)(2,1)}, u32[]{:S(2)}, u32[]{:S(2)}) collective-permute-start(bf16[128,1792]{1,0:T(8,128)(2,1)} %constant_dynamic-slice_fusion), channel_id=1, source_target_pairs={{0,0},{1,4},{2,8},{3,12},{4,1},{5,5},{6,9},{7,13},{8,2},{9,6},{10,... | collective-permute-start | bytes 1376264 | tf_op jit(solution)/shard_map/ppermute | solution.py:56
  92.3 0.0 all-gather.2.cloned.1.call-update
  92.4 0.0 reduce-scatter.9.cloned.1.call-start
  92.4 32.1 %collective-permute-done.4 = bf16[128,6528]{1,0:T(8,128)(2,1)} collective-permute-done((bf16[128,6528]{1,0:T(8,128)(2,1)}, bf16[128,6528]{1,0:T(8,128)(2,1)}, u32[]{:S(2)}, u32[]{:S(2)}) %collective-permute-start.4) | collective-permute-done | bytes 1671200 | tf_op jit(solution)/shard_map/ppermute | solution.py:73
  124.6 1.6 constant_dynamic-update-slice_fusion.7
  126.1 1.8 constant_dynamic-update-slice_fusion.6
  127.9 0.2 constant_dynamic-update-slice_fusion.5
  128.2 0.4 constant_dynamic-update-slice_fusion.4
  128.5 1.8 constant_dynamic-update-slice_fusion.3
  130.4 1.7 constant_dynamic-update-slice_fusion.2
  132.1 0.2 constant_dynamic-update-slice_fusion.1
  132.3 0.4 constant_dynamic-update-slice_fusion
  132.7 4.4 %fusion.2 = bf16[512,384]{1,0:T(8,128)(2,1)} fusion(bf16[384,6528]{1,0:T(8,128)(2,1)S(1)} %bitcast.15, bf16[1024,6528]{1,0:T(8,128)(2,1)S(1)} %constant_dynamic-update-slice_fusion, s32[]{:T(128)S(6)} %select_n.35), kind=kOutput, calls=%fused_computation.4 | convolution fusion | flops 2567110656 | bytes 12091396 | tf_op jit(solution)/shard_map/dot_general | solution.py:10
  137.1 0.0 reduce-scatter.9.cloned.1.call-update
  137.2 0.0 reduce-scatter.5.cloned.1.call-start
  137.2 31.4 %all-gather.2.cloned.1.call-done = bf16[512,1792]{1,0:T(8,128)(2,1)} async-done(((bf16[128,1792]{1,0:T(8,128)(2,1)}), bf16[512,1792]{1,0:T(8,128)(2,1)}) %all-gather.2.cloned.1.call-update) | async-done | bytes 1835024 | tf_op jit(solution)/shard_map/all_gather | solution.py:60
  168.6 3.5 fusion.15
  172.1 0.0 reduce-scatter.5.cloned.1.call-update
  172.2 0.0 reduce-scatter.11.cloned.1.call-start
  172.2 19.8 %reduce-scatter.9.cloned.1.call-done = bf16[128,384]{1,0:T(8,128)(2,1)} async-done(((bf16[512,384]{1,0:T(8,128)(2,1)}), bf16[128,384]{1,0:T(8,128)(2,1)}) %reduce-scatter.9.cloned.1.call-update) | async-done | bytes 98320 | tf_op jit(solution)/shard_map/reduce_scatter | solution.py:80
  192.0 1.5 collective-permute-start.5
  193.5 22.5 %reduce-scatter.5.cloned.1.call-done = f32[128,384]{1,0:T(8,128)} async-done(((f32[512,384]{1,0:T(8,128)}), f32[128,384]{1,0:T(8,128)}) %reduce-scatter.5.cloned.1.call-update) | async-done | bytes 196624 | tf_op jit(solution)/shard_map/reduce_scatter | solution.py:62
  216.0 1.0 multiply_reduce_fusion
  217.1 6.4 %all-reduce = (f32[128,1]{0,1:T(1,128)S(1)}, f32[128]{0:T(128)S(1)}) all-reduce(f32[128,1]{0,1:T(1,128)S(1)} %bitcast.13, f32[128]{0:T(128)S(1)} %get-tuple-element.2), channel_id=1, replica_groups=mesh['groups'=2,'dp'=4,'mp'=4] {'mp'}, use_global_device_ids=true, to_apply=%region_2.3 | all-reduce | flops 256 | bytes 2048 | tf_op jit(solution)/shard_map/psum | solution.py:63
  223.5 1.1 subtract_convert_fusion
  224.6 11.9 %all_gather.11 = bf16[512,384]{1,0:T(8,128)(2,1)S(1)} all-gather(bf16[128,384]{1,0:T(8,128)(2,1)S(1)} %get-tuple-element.6), channel_id=1, replica_groups=mesh['groups'=2,'dp'=4,'mp'=4] {'dp'}, dimensions={0}, use_global_device_ids=true | all-gather | bytes 491520 | tf_op jit(solution)/shard_map/all_gather | solution.py:86
  236.5 2.4 convolution_convert_fusion
  239.0 0.0 reduce-scatter.11.cloned.1.call-update
  239.0 0.0 reduce-scatter.7.cloned.1.call-start
  239.0 0.7 collective-permute-start.1
  239.7 0.7 fusion.8
  240.4 16.0 %all_gather.10 = bf16[512,384]{1,0:T(8,128)(2,1)S(1)} all-gather(bf16[128,384]{1,0:T(8,128)(2,1)S(1)} %collective-permute-done.1), channel_id=1, replica_groups=mesh['groups'=2,'dp'=4,'mp'=4] {'mp'}, dimensions={0}, use_global_device_ids=true | all-gather | bytes 491520 | tf_op jit(solution)/shard_map/all_gather | solution.py:66
  256.5 8.0 %multiply_convert_fusion = bf16[512,6528]{1,0:T(8,128)(2,1)} fusion(bf16[512,384]{1,0:T(8,128)(2,1)S(1)} %all_gather.10, bf16[384,6528]{1,0:T(8,128)(2,1)} %param.9, f32[6528]{0:T(1024)S(1)} %fusion.8), kind=kOutput, calls=%fused_computation | convolution fusion | flops 2573598720 | bytes 12117504 | tf_op jit(solution)/shard_map/dot_general | solution.py:67
  264.5 0.0 reduce-scatter.7.cloned.1.call-update
  264.5 8.1 %reduce-scatter.11.cloned.1.call-done = bf16[128,1792]{1,0:T(8,128)(2,1)} async-done(((bf16[512,1792]{1,0:T(8,128)(2,1)}), bf16[128,1792]{1,0:T(8,128)(2,1)}) %reduce-scatter.11.cloned.1.call-update) | async-done | bytes 458768 | tf_op jit(solution)/shard_map/reduce_scatter | solution.py:89
  272.6 1.7 collective-permute-start.6
  274.2 132.7 %reduce-scatter.7.cloned.1.call-done = bf16[128,6528]{1,0:T(8,128)(2,1)} async-done(((bf16[512,6528]{1,0:T(8,128)(2,1)}), bf16[128,6528]{1,0:T(8,128)(2,1)}) %reduce-scatter.7.cloned.1.call-update) | async-done | bytes 1671184 | tf_op jit(solution)/shard_map/reduce_scatter | solution.py:77
  407.0 0.8 copy.16
  (18 shorter events, 0.1 us)
Async XLA Ops:
  7.2 79.3 %copy-start = (bf16[128,7168]{1,0:T(8,128)(2,1)S(1)}, bf16[128,7168]{1,0:T(8,128)(2,1)}, u32[]{:S(2)}) copy-start(bf16[128,7168]{1,0:T(8,128)(2,1)} %param.6) | copy-start | bytes 5505028
  7.2 161.5 %all-gather.2.cloned.1.call-start = ((), (), s32[]{:S(2)}) async-start(), calls=%async_computation.4 | async-start | bytes 2293760 | tf_op jit(solution)/shard_map/all_gather | solution.py:60
  11.0 37.4 %collective-permute-start.2 = (bf16[128,6528]{1,0:T(8,128)(2,1)S(1)}, bf16[128,6528]{1,0:T(8,128)(2,1)S(1)}, u32[]{:S(2)}, u32[]{:S(2)}) collective-permute-start(bf16[128,6528]{1,0:T(8,128)(2,1)S(1)} %broadcast_multiply_fusion), channel_id=1, source_target_pairs={{0,4},{4,8},{8,12},{12,0},{1,5},{5,9},{9,13},{13,1},{2,6},{6,10},{... | collective-permute-start | bytes 5013512 | tf_op jit(solution)/shard_map/ppermute | solution.py:73
  48.4 38.0 %collective-permute-start.3 = (bf16[128,6528]{1,0:T(8,128)(2,1)S(1)}, bf16[128,6528]{1,0:T(8,128)(2,1)}, u32[]{:S(2)}, u32[]{:S(2)}) collective-permute-start(bf16[128,6528]{1,0:T(8,128)(2,1)S(1)} %collective-permute-done.2), channel_id=1, source_target_pairs={{0,4},{4,8},{8,12},{12,0},{1,5},{5,9},{9,13},{13,1},{2,6},{6,10},{... | collective-permute-start | bytes 5013512 | tf_op jit(solution)/shard_map/ppermute | solution.py:73
  86.5 38.1 %collective-permute-start.4 = (bf16[128,6528]{1,0:T(8,128)(2,1)}, bf16[128,6528]{1,0:T(8,128)(2,1)}, u32[]{:S(2)}, u32[]{:S(2)}) collective-permute-start(bf16[128,6528]{1,0:T(8,128)(2,1)} %collective-permute-done.3), channel_id=1, source_target_pairs={{0,4},{4,8},{8,12},{12,0},{1,5},{5,9},{9,13},{13,1},{2,6},{6,10},{... | collective-permute-start | bytes 5013512 | tf_op jit(solution)/shard_map/ppermute | solution.py:73
  87.3 5.1 %collective-permute-start = (bf16[128,1792]{1,0:T(8,128)(2,1)}, bf16[128,1792]{1,0:T(8,128)(2,1)}, u32[]{:S(2)}, u32[]{:S(2)}) collective-permute-start(bf16[128,1792]{1,0:T(8,128)(2,1)} %constant_dynamic-slice_fusion), channel_id=1, source_target_pairs={{0,0},{1,4},{2,8},{3,12},{4,1},{5,5},{6,9},{7,13},{8,2},{9,6},{10,... | collective-permute-start | bytes 1376264 | tf_op jit(solution)/shard_map/ppermute | solution.py:56
  92.4 99.6 %reduce-scatter.9.cloned.1.call-start = ((), (), s32[]{:S(2)}) async-start(), calls=%async_computation.7 | async-start | bytes 491520 | tf_op jit(solution)/shard_map/reduce_scatter | solution.py:80
  126.1 2.0 copy-start.1
  128.1 4.6 %slice-start = ((s8[5013504]{0:T(1024)(128)(4,1)}), s8[4194304]{0:T(1024)(128)(4,1)S(1)}, s32[]{:S(2)}) async-start(s8[5013504]{0:T(1024)(128)(4,1)} %bitcast.14), calls=%async_computation.9 | async-start | bytes 8388608
  130.4 2.3 slice-start.1
  132.7 35.9 %copy-start.2 = (bf16[1792,384]{1,0:T(8,128)(2,1)S(1)}, bf16[1792,384]{1,0:T(8,128)(2,1)}, u32[]{:S(2)}) copy-start(bf16[1792,384]{1,0:T(8,128)(2,1)} %param.7) | copy-start | bytes 4128772
  137.1 78.9 %copy-start.3 = (f32[384]{0:T(512)S(1)}, f32[384]{0:T(512)}, u32[]{:S(2)}) copy-start(f32[384]{0:T(512)} %param.8) | copy-start | bytes 4612
  137.2 78.9 %reduce-scatter.5.cloned.1.call-start = ((), (), s32[]{:S(2)}) async-start(), calls=%async_computation.5 | async-start | bytes 983040 | tf_op jit(solution)/shard_map/reduce_scatter | solution.py:62
  172.2 100.4 %reduce-scatter.11.cloned.1.call-start = ((), (), s32[]{:S(2)}) async-start(), calls=%async_computation.8 | async-start | bytes 2293760 | tf_op jit(solution)/shard_map/reduce_scatter | solution.py:89
  192.0 24.0 %collective-permute-start.5 = (bf16[128,384]{1,0:T(8,128)(2,1)}, bf16[128,384]{1,0:T(8,128)(2,1)S(1)}, u32[]{:S(2)}, u32[]{:S(2)}) collective-permute-start(bf16[128,384]{1,0:T(8,128)(2,1)} %reduce-scatter.9.cloned.1.call-done), channel_id=1, source_target_pairs={{0,0},{1,4},{2,8},{3,12},{4,1},{5,5},{6,9},{7,13},{8,2},{9,6},{10,... | collective-permute-start | bytes 294920 | tf_op jit(solution)/shard_map/ppermute | solution.py:56
  239.0 168.0 %reduce-scatter.7.cloned.1.call-start = ((), (), s32[]{:S(2)}) async-start(), calls=%async_computation.6 | async-start | bytes 8355840 | tf_op jit(solution)/shard_map/reduce_scatter | solution.py:77
  239.0 1.4 collective-permute-start.1
  272.6 1.7 collective-permute-start.6
Sparse Core Ops, SparseCore 0:
  92.5 76.0 all-gather.1
  171.7 20.2 reduce-scatter.8
  194.9 21.1 reduce-scatter.4
  239.1 33.4 reduce-scatter.10
  275.3 131.5 reduce-scatter.6
